TPU v7x, 32 devices: a whole 2x2x4 slice. The times are simulated.
32 devices in a mesh: dp: 8 (over y, x, core), fsdp: 4 (over z).
Axes of the slice: x: 2, y: 2, z: 4, core: 2. Of those that a mesh axis runs over, the one named last changes fastest.
Arguments:
- hidden: bfloat16 [16384, 8192], P('dp', 'fsdp'), may hold values from -50 to 50
- logit_grad: bfloat16 [16384, 256], P('dp'), may hold values from -20 to 20
- master: float32 [256, 8192], P('dp', 'fsdp'), may hold values from -6 to 6
- moment_one: float32 [256, 8192], P('dp', 'fsdp'), may hold values from -4 to 4
- moment_two: float32 [256, 8192], P('dp', 'fsdp'), may hold values from 0.25 to 4
Outputs:
- new_rows: bfloat16 [256, 8192], P(None, 'fsdp')
- new_master: float32 [256, 8192], P('dp', 'fsdp')
- new_one: float32 [256, 8192], P('dp', 'fsdp')
- new_two: float32 [256, 8192], P('dp', 'fsdp')
All inputs are finite; a program needn't handle non-finite values.
Results may differ from a plain program's by a relative error of at most 0.012.
Values may be sent and summed in bfloat16 or wider, within the bound.
A program may use at most 64 MiB of HBM per device.

v0:
```python
import jax
import jax.numpy as jnp
from jax import lax
from jax.sharding import PartitionSpec as P


def shards(hidden, logit_grad, master, moment_one, moment_two):
    columns_here = master.shape[1]
    total_rows = logit_grad.shape[1]
    width = columns_here * lax.axis_size("fsdp")
    part = lax.dot_general(
        logit_grad, hidden, (((0,), (0,)), ((), ())), preferred_element_type=jnp.float32
    )
    grad = lax.psum_scatter(
        lax.optimization_barrier(part.astype(jnp.bfloat16))
        .astype(jnp.float32)
        .astype(jnp.bfloat16),
        "dp",
        scatter_dimension=0,
        tiled=True,
    ).astype(jnp.float32)
    sumsq = lax.psum(jnp.sum(grad * grad), ("dp", "fsdp"))
    rms_value = jnp.sqrt(sumsq / (total_rows * width))
    factor = jnp.minimum(1.0, 1.0 / rms_value)
    clipped = factor * grad
    new_one = 0.9 * moment_one + 0.1 * clipped
    new_two = 0.95 * moment_two + 0.05 * clipped * clipped
    first = new_one / (1.0 - 0.9**10)
    second = new_two / (1.0 - 0.95**10)
    new_master = master - 0.05 * (first / (jnp.sqrt(second) + 1e-08) + 0.1 * master)
    own_rows = new_master.astype(jnp.bfloat16)
    new_rows = lax.all_gather(own_rows, "dp", axis=0, tiled=True)
    return (new_rows, new_master, new_one, new_two)


def solution(mesh):
    placed = (P("dp", "fsdp"), P("dp", None), P("dp", "fsdp"), P("dp", "fsdp"), P("dp", "fsdp"))
    return jax.shard_map(
        shards,
        mesh=mesh,
        in_specs=placed,
        out_specs=(P(None, "fsdp"), P("dp", "fsdp"), P("dp", "fsdp"), P("dp", "fsdp")),
        check_vma=False,
    )
```

profile of v0, /device:TPU:0, one launch (start us, length us, event | category | flops | bytes accessed | tf_op | source)
XLA Modules:
  0.0 131.3 jit_solution(7110176912480280082)
XLA Ops:
  7.2 0.0 copy-start
  7.2 0.0 copy-start.3
  7.2 0.0 copy-start.2
  7.2 0.0 copy-start.1
  7.2 0.0 reduce-scatter.2.cloned.1.call-start
  7.3 1.1 copy-done
  8.4 6.7 %convolution_convert_fusion = bf16[256,2048]{1,0:T(8,128)(2,1)} fusion(bf16[2048,256]{1,0:T(8,128)(2,1)S(1)} %copy-done, bf16[2048,2048]{1,0:T(8,128)(2,1)} %param.5), kind=kOutput, calls=%fused_computation | convolution fusion | flops 2148007936 | bytes 10485760 | tf_op jit(solution)/shard_map/dot_general | solution.py:11
  15.1 0.0 reduce-scatter.2.cloned.1.call-update
  15.1 0.0 all-gather.2.cloned.1.call-start
  15.2 38.8 %reduce-scatter.2.cloned.1.call-done = bf16[32,2048]{1,0:T(8,128)(2,1)} async-done(((bf16[256,2048]{1,0:T(8,128)(2,1)}), bf16[32,2048]{1,0:T(8,128)(2,1)}) %reduce-scatter.2.cloned.1.call-update) | async-done | bytes 131088 | tf_op jit(solution)/shard_map/reduce_scatter | solution.py:14
  54.0 1.6 %fusion.2 = f32[]{:T(128)} fusion(bf16[32,2048]{1,0:T(8,128)(2,1)} %reduce-scatter.2.cloned.1.call-done), kind=kLoop, calls=%fused_computation.6 | loop fusion | flops 196607 | bytes 131076 | tf_op jit(solution)/shard_map/reduce_sum | solution.py:22
  55.5 39.5 %psum.7 = f32[]{:T(128)} all-reduce(f32[]{:T(128)} %fusion.2), channel_id=1, replica_groups=mesh['dp'=8,'fsdp'=4] {'dp','fsdp'}, use_global_device_ids=true, to_apply=%region_2.0 | all-reduce | flops 1 | bytes 8 | tf_op jit(solution)/shard_map/psum | solution.py:22
  95.7 0.0 copy-done.3
  95.7 0.0 copy-done.2
  95.7 0.0 copy-done.1
  95.7 2.0 %fusion.4 = (bf16[32,2048]{1,0:T(8,128)(2,1)}, f32[32,2048]{1,0:T(8,128)}, f32[32,2048]{1,0:T(8,128)}, f32[32,2048]{1,0:T(8,128)}) fusion(f32[32,2048]{1,0:T(8,128)S(1)} %copy-done.1, bf16[32,2048]{1,0:T(8,128)(2,1)} %reduce-scatter.2.cloned.1.call-done, f32[]{:T(128)S(6)} %min.3, f32[32,2048]{1,0:T(8,128)S(1)} %copy-done.2, f32[32,2048]{1,0:T(8,128)S(1)} %copy-done.3), kind=kLoop, calls=%fused_computation.9 | loop fusion | flops 1179648 | bytes 1835012 | tf_op jit(solution)/shard_map/convert_element_type | solution.py:31
  97.7 0.0 all-gather.2.cloned.1.call-update
  97.7 24.4 %all-gather.2.cloned.1.call-done = bf16[256,2048]{1,0:T(8,128)(2,1)} async-done(((bf16[32,2048]{1,0:T(8,128)(2,1)}), bf16[256,2048]{1,0:T(8,128)(2,1)}) %all-gather.2.cloned.1.call-update) | async-done | bytes 1048592 | tf_op jit(solution)/shard_map/all_gather | solution.py:32
  122.2 2.3 %copy.10 = bf16[256,2048]{1,0:T(8,128)(2,1)} copy(bf16[256,2048]{1,0:T(8,128)(2,1)} %all-gather.2.cloned.1.call-done) | data formatting | bytes 2097152
Async XLA Ops:
  7.2 1.2 copy-start
  7.2 88.5 %copy-start.3 = (f32[32,2048]{1,0:T(8,128)S(1)}, f32[32,2048]{1,0:T(8,128)}, u32[]{:S(2)}) copy-start(f32[32,2048]{1,0:T(8,128)} %param.9) | copy-start | bytes 786436
  7.2 88.5 %copy-start.2 = (f32[32,2048]{1,0:T(8,128)S(1)}, f32[32,2048]{1,0:T(8,128)}, u32[]{:S(2)}) copy-start(f32[32,2048]{1,0:T(8,128)} %param.8) | copy-start | bytes 786436
  7.2 88.5 %copy-start.1 = (f32[32,2048]{1,0:T(8,128)S(1)}, f32[32,2048]{1,0:T(8,128)}, u32[]{:S(2)}) copy-start(f32[32,2048]{1,0:T(8,128)} %param.7) | copy-start | bytes 786436
  7.2 46.7 %reduce-scatter.2.cloned.1.call-start = ((), (), s32[]{:S(2)}) async-start(), calls=%async_computation.1 | async-start | bytes 1179648 | tf_op jit(solution)/shard_map/reduce_scatter | solution.py:14
  15.1 107.0 %all-gather.2.cloned.1.call-start = ((), (), s32[]{:S(2)}) async-start(), calls=%async_computation.2 | async-start | bytes 1179648 | tf_op jit(solution)/shard_map/all_gather | solution.py:32
Sparse Core Ops, SparseCore 0:
  15.2 38.6 reduce-scatter.1
  97.8 24.2 all-gather.1
where the time goes:
time: 132 us; the launch traced here: 131 us
  waiting for transfers between devices  63.3 us (48%)
  blocking collectives  39.5 us (30%)
  between operations  14.8 us (11%)
  matrix products  6.7 us (5%)
  other arithmetic  3.53 us (3%)
  local copies, waits for them, and re-layouts  3.46 us (3%)
    psum x1, blocking collectives, shards(): sumsq = lax.psum(jnp.sum(grad * grad), ('dp', 'fsdp'))  39.5 us
    reduce_scatter x1, waiting for transfers between devices, shards(): lax.psum_scatter(lax.optimization_barrier(part.astype(jnp.bfloat16)).asty...  38.8 us
    all_gather x1, waiting for transfers between devices, shards(): new_rows = lax.all_gather(own_rows, 'dp', axis=0, tiled=True)  24.4 us
    dot_general x1, matrix products, shards(): lax.dot_general(logit_grad, hidden, (((0,), (0,)), ((), ())), preferred_e...  6.7 us
    unnamed x9, local copies, waits for them, and re-layouts  3.46 us
  transfers between devices with their start and end apart: 2, of which 2 were waited for; matrix products, arithmetic and copies ran while one was open for 0% of the time, Pallas kernels for 0%

commit v1 on v0

v1 whole, which is shorter than its diff:
```python
import functools

import jax
import jax.numpy as jnp
from jax import lax
from jax.experimental import pallas as pl
from jax.experimental.pallas import tpu as pltpu
from jax.sharding import PartitionSpec as P

MESH = pl.DeviceIdType.MESH
LOAD_CHUNKS = 4
GATHER_CHUNKS = 2


def pieces(width, wanted):
    count = wanted
    while count > 1 and width % (count * 128):
        count -= 1
    return count


def kernel(
    n, depth, chunks, gathers,
    hid, lgr, mas, one, two,
    rows_out, mas_out, one_out, two_out,
    lgr_v, lgt_v, hid_v, mas_v, one_v, two_v,
    stage, paired, sums, arrived, grad, sq_all, gath,
    hid_sem, lgr_sem, state_sem, pair_send, pair_recv, chip_send, chip_recv,
    sq_send, sq_recv, ag_send, ag_recv, relay_send, relay_recv, rows_sem, out_sem,
):
    chips = n // 2
    total = n * depth
    rows, width = grad.shape
    dp, fs = lax.axis_index("dp"), lax.axis_index("fsdp")
    chip, core = dp // 2, dp % 2
    other = 1 - core
    me = dp * depth + fs
    wc, wa = width // chunks, width // gathers

    lgr_copy = pltpu.make_async_copy(lgr, lgr_v, lgr_sem)
    lgr_copy.start()
    loads = []
    for j in range(chunks):
        load = pltpu.make_async_copy(hid.at[:, pl.ds(j * wc, wc)], hid_v.at[j], hid_sem.at[j])
        load.start()
        loads.append(load)
    states = []
    for i, (src, dst) in enumerate(((mas, mas_v), (one, one_v), (two, two_v))):
        load = pltpu.make_async_copy(src, dst, state_sem.at[i])
        load.start()
        states.append(load)

    def each_other_device(act):
        def visit(i):
            index = (me + i) % total
            act((index // depth, index % depth))

        if total <= 64:
            for i in range(1, total):
                visit(i)
        else:
            lax.fori_loop(1, total, lambda i, carry: (visit(i), carry)[1], 0)

    barrier = pltpu.get_barrier_semaphore()
    each_other_device(
        lambda to: pl.semaphore_signal(barrier, inc=1, device_id=to, device_id_type=MESH)
    )

    lgr_copy.wait()
    lgt_v[...] = lgr_v[...].T

    def remote(src, dst, send, recv, to):
        return pltpu.make_async_remote_copy(
            src_ref=src, dst_ref=dst, send_sem=send, recv_sem=recv, device_id=to, device_id_type=MESH
        )

    partner = (2 * chip + other, fs)
    others = [(chip + o) % chips for o in range(1, chips)]

    def pair_copy(j):
        return remote(stage.at[j, other], paired.at[j], pair_send.at[j], pair_recv.at[j], partner)

    def chip_copy(j, q, slot):
        return remote(
            sums.at[j, q], arrived.at[j, slot], chip_send.at[j, q], chip_recv.at[j, slot],
            (2 * q + core, fs),
        )

    def chip_sum(j):
        pair_copy(j).wait_recv()
        for q in others:
            both = stage[j, core, q].astype(jnp.float32) + paired[j, q].astype(jnp.float32)
            sums[j, q] = both.astype(jnp.bfloat16)
            chip_copy(j, q, chip).start()
        grad[:, pl.ds(j * wc, wc)] = stage[j, core, chip].astype(jnp.float32) + paired[
            j, chip
        ].astype(jnp.float32)

    for j in range(chunks):
        loads[j].wait()
        part = jnp.dot(lgt_v[...], hid_v[j], preferred_element_type=jnp.float32)
        part = part.astype(jnp.bfloat16)
        for q in range(chips):
            for c in range(2):
                d = 2 * q + c
                stage[j, c, q] = part[d * rows : (d + 1) * rows, :]
        if j == 0:
            pl.semaphore_wait(barrier, total - 1)
        pair_copy(j).start()
        if j > 0:
            chip_sum(j - 1)
    chip_sum(chunks - 1)

    squares = jnp.zeros((1, 128), jnp.float32)
    for j in range(chunks):
        span = pl.ds(j * wc, wc)
        value = grad[:, span]
        for q in others:
            chip_copy(j, q, q).wait_recv()
            value = value + arrived[j, q].astype(jnp.float32)
        grad[:, span] = value
        column = jnp.sum(value * value, axis=0, keepdims=True)
        for s in range(wc // 128):
            squares = squares + column[:, s * 128 : (s + 1) * 128]

    sq_all[me] = squares
    each_other_device(
        lambda to: remote(sq_all.at[me], sq_all.at[me], sq_send, sq_recv, to).start()
    )
    for load in states:
        load.wait()
    everyone = sq_all.at[pl.ds(0, total - 1)]
    pltpu.make_async_copy(everyone, everyone, sq_recv).wait()
    sumsq = jnp.sum(jnp.sum(sq_all[...], axis=0), axis=1, keepdims=True)
    rms = jnp.sqrt(sumsq / (rows * n * width * depth))
    factor = jnp.where(rms > 1.0, 1.0 / rms, 1.0)

    def cols(k):
        return pl.ds(k * wa, wa)

    def gather_copy(k, d, to, send, recv):
        block = gath.at[d, :, cols(k)]
        return remote(block, block, send, recv, to)

    def direct(k, source, q):
        return gather_copy(k, 2 * source + core, (2 * q + core, fs), ag_send.at[k, q], ag_recv.at[k, source])

    def relay(k, q, side):
        return gather_copy(k, 2 * q + side, partner, relay_send.at[k, q], relay_recv.at[k, q])

    def put_rows(k, d):
        pltpu.make_async_copy(
            gath.at[d, :, cols(k)],
            rows_out.at[pl.ds(pl.multiple_of(d * rows, rows), rows), cols(k)],
            rows_sem,
        ).start()

    for k in range(gathers):
        span = cols(k)
        clipped = factor * grad[:, span]
        new_one = 0.9 * one_v[:, span] + 0.1 * clipped
        new_two = 0.95 * two_v[:, span] + 0.05 * clipped * clipped
        first = new_one / (1.0 - 0.9**10)
        second = new_two / (1.0 - 0.95**10)
        held = mas_v[:, span]
        new_master = held - 0.05 * (first / (jnp.sqrt(second) + 1e-08) + 0.1 * held)
        gath[dp, :, span] = new_master.astype(jnp.bfloat16)
        for q in others:
            direct(k, chip, q).start()
        relay(k, chip, core).start()
        put_rows(k, dp)
        one_v[:, span] = new_one
        two_v[:, span] = new_two
        mas_v[:, span] = new_master
    outs = []
    for i, (src, dst) in enumerate(((mas_v, mas_out), (one_v, one_out), (two_v, two_out))):
        out = pltpu.make_async_copy(src, dst, out_sem.at[i])
        out.start()
        outs.append(out)
    for k in range(gathers):
        for q in others:
            direct(k, q, q).wait_recv()
            relay(k, q, core).start()
            put_rows(k, 2 * q + core)
    for k in range(gathers):
        for q in [chip] + others:
            relay(k, q, other).wait_recv()
            put_rows(k, 2 * q + other)

    for j in range(chunks):
        pair_copy(j).wait_send()
        for q in others:
            chip_copy(j, q, chip).wait_send()
    pltpu.make_async_copy(everyone, everyone, sq_send).wait()
    for k in range(gathers):
        for q in others:
            direct(k, chip, q).wait_send()
            relay(k, q, core).wait_send()
        relay(k, chip, core).wait_send()
    for out in outs:
        out.wait()
    pltpu.make_async_copy(rows_out, rows_out, rows_sem).wait()


def shards(n, depth, hidden, logit_grad, master, moment_one, moment_two):
    tokens, width = hidden.shape
    slab = logit_grad.shape[1]
    rows = master.shape[0]
    chips = n // 2
    chunks = pieces(width, LOAD_CHUNKS)
    gathers = pieces(width, GATHER_CHUNKS)
    wc = width // chunks
    f32, bf16 = jnp.float32, jnp.bfloat16
    state = jax.ShapeDtypeStruct((rows, width), f32)
    dma = pltpu.SemaphoreType.DMA
    anywhere = pl.BlockSpec(memory_space=pl.ANY)
    return pl.pallas_call(
        functools.partial(kernel, n, depth, chunks, gathers),
        out_shape=(jax.ShapeDtypeStruct((slab, width), bf16), state, state, state),
        in_specs=[anywhere] * 5,
        out_specs=(anywhere,) * 4,
        scratch_shapes=[
            pltpu.VMEM((tokens, slab), bf16),
            pltpu.VMEM((slab, tokens), bf16),
            pltpu.VMEM((chunks, tokens, wc), bf16),
            pltpu.VMEM((rows, width), f32),
            pltpu.VMEM((rows, width), f32),
            pltpu.VMEM((rows, width), f32),
            pltpu.VMEM((chunks, 2, chips, rows, wc), bf16),
            pltpu.VMEM((chunks, chips, rows, wc), bf16),
            pltpu.VMEM((chunks, chips, rows, wc), bf16),
            pltpu.VMEM((chunks, chips, rows, wc), bf16),
            pltpu.VMEM((rows, width), f32),
            pltpu.VMEM((n * depth, 1, 128), f32),
            pltpu.VMEM((n, rows, width), bf16),
            dma((chunks,)),
            dma,
            dma((3,)),
            dma((chunks,)),
            dma((chunks,)),
            dma((chunks, chips)),
            dma((chunks, chips)),
            dma,
            dma,
            dma((gathers, chips)),
            dma((gathers, chips)),
            dma((gathers, chips)),
            dma((gathers, chips)),
            dma,
            dma((3,)),
        ],
        compiler_params=pltpu.CompilerParams(
            collective_id=0, has_side_effects=True, vmem_limit_bytes=60 * 1024 * 1024
        ),
    )(hidden, logit_grad, master, moment_one, moment_two)


def solution(mesh):
    placed = (P("dp", "fsdp"), P("dp", None), P("dp", "fsdp"), P("dp", "fsdp"), P("dp", "fsdp"))
    return jax.shard_map(
        functools.partial(shards, mesh.shape["dp"], mesh.shape["fsdp"]),
        mesh=mesh,
        in_specs=placed,
        out_specs=(P(None, "fsdp"), P("dp", "fsdp"), P("dp", "fsdp"), P("dp", "fsdp")),
        check_vma=False,
    )
```

time: 132 us -> 40 us (0.30)
  waiting for transfers between devices: 63.3 us -> 0 us
  blocking collectives: 39.5 us -> 0 us
  Pallas kernels: 0 us -> 31.3 us
  between operations: 14.8 us -> 0.64 us
  matrix products: 6.7 us -> 0 us
  local copies, waits for them, and re-layouts: 3.46 us -> 7.31 us
  other arithmetic: 3.53 us -> 0 us
    psum x1 -> x0, blocking collectives: 39.5 us -> none  [shards(): sumsq = lax.psum(jnp.sum(grad * grad), ('dp', 'fsdp'))]
    reduce_scatter x1 -> x0, waiting for transfers between devices: 38.8 us -> none  [shards(): lax.psum_scatter(lax.optimization_barrier(part.astype(jnp.bfloat16)).asty...]
    pallas_call x0 -> x1, Pallas kernels: none -> 31.3 us  [shards(): pl.pallas_call(functools.partial(kernel, n, depth, chunks, gathers), out_...]
    all_gather x1 -> x0, waiting for transfers between devices: 24.4 us -> none  [shards(): new_rows = lax.all_gather(own_rows, 'dp', axis=0, tiled=True)]
    dot_general x1 -> x0, matrix products: 6.7 us -> none  [shards(): lax.dot_general(logit_grad, hidden, (((0,), (0,)), ((), ())), preferred_e...]
    unnamed x9 -> x4, local copies, waits for them, and re-layouts: 3.46 us -> 7.31 us
    convert_element_type x1 -> x0, other arithmetic: 1.96 us -> none  [shards(): own_rows = new_master.astype(jnp.bfloat16)]
    reduce_sum x1 -> x0, other arithmetic: 1.58 us -> none  [shards(): sumsq = lax.psum(jnp.sum(grad * grad), ('dp', 'fsdp'))]
  transfers between devices with their start and end apart: 2 -> 0, of which waited for: 2 -> 0; matrix products, arithmetic and copies ran while one was open for 0% -> 0% of each run, Pallas kernels for 0% -> 0%
where the time goes in v1:
time: 40 us; the launch traced here: 39.2 us
  Pallas kernels  31.3 us (78%)
  local copies, waits for them, and re-layouts  7.31 us (18%)
  between operations  0.64 us (2%)
    pallas_call x1, Pallas kernels, shards(): pl.pallas_call(functools.partial(kernel, n, depth, chunks, gathers), out_...  31.3 us
    unnamed x4, local copies, waits for them, and re-layouts  7.31 us

profile of v1, /device:TPU:0, one launch (start us, length us, event | category | flops | bytes accessed | tf_op | source)
XLA Modules:
  0.0 39.2 jit_solution(14169550271158994947)
XLA Ops:
  0.6 31.3 %shard_map.84 = (bf16[256,2048]{1,0:T(8,128)(2,1)}, f32[32,2048]{1,0:T(8,128)}, f32[32,2048]{1,0:T(8,128)}, f32[32,2048]{1,0:T(8,128)}) custom-call(bf16[2048,2048]{1,0:T(8,128)(2,1)} %hid.1, bf16[2048,256]{1,0:T(8,128)(2,1)} %lgr.1, f32[32,2048]{1,0:T(8,128)} %mas.1, f32[32,2048]{1,0:T(8,128)} %one.1, f32[32,2048]{1,0:T(8,128)} %two.1), custom_call_target="tpu_custom_call" | custom-call | tf_op jit(solution)/shard_map/pallas_call | solution.py:217
  31.9 2.3 %copy.13 = bf16[256,2048]{1,0:T(8,128)(2,1)} copy(bf16[256,2048]{1,0:T(8,128)(2,1)} %get-tuple-element.8) | data formatting | bytes 2097152
  34.2 1.7 %copy.14 = f32[32,2048]{1,0:T(8,128)} copy(f32[32,2048]{1,0:T(8,128)} %get-tuple-element.9) | data formatting | bytes 524288
  35.9 1.7 %copy.15 = f32[32,2048]{1,0:T(8,128)} copy(f32[32,2048]{1,0:T(8,128)} %get-tuple-element.10) | data formatting | bytes 524288
  37.6 1.7 %copy.16 = f32[32,2048]{1,0:T(8,128)} copy(f32[32,2048]{1,0:T(8,128)} %get-tuple-element.11) | data formatting | bytes 524288

commit v2 on v1

--- a/solution.py
+++ b/solution.py
@@ -10,6 +10,7 @@
 MESH = pl.DeviceIdType.MESH
 LOAD_CHUNKS = 4
 GATHER_CHUNKS = 2
+VMEM_BYTES = 67_043_328
 
 
 def pieces(width, wanted):
@@ -24,9 +25,9 @@
     hid, lgr, mas, one, two,
     rows_out, mas_out, one_out, two_out,
     lgr_v, lgt_v, hid_v, mas_v, one_v, two_v,
-    stage, paired, sums, arrived, grad, sq_all, gath,
+    stage, paired, sums, arrived, grad, sq_all,
     hid_sem, lgr_sem, state_sem, pair_send, pair_recv, chip_send, chip_recv,
-    sq_send, sq_recv, ag_send, ag_recv, relay_send, relay_recv, rows_sem, out_sem,
+    sq_send, sq_recv, ag_send, ag_recv, relay_send, relay_recv,
 ):
     chips = n // 2
     total = n * depth
@@ -138,8 +139,11 @@
     def cols(k):
         return pl.ds(k * wa, wa)
 
+    def rows_of(d):
+        return pl.ds(pl.multiple_of(d * rows, rows), rows)
+
     def gather_copy(k, d, to, send, recv):
-        block = gath.at[d, :, cols(k)]
+        block = rows_out.at[rows_of(d), cols(k)]
         return remote(block, block, send, recv, to)
 
     def direct(k, source, q):
@@ -147,13 +151,6 @@
 
     def relay(k, q, side):
         return gather_copy(k, 2 * q + side, partner, relay_send.at[k, q], relay_recv.at[k, q])
-
-    def put_rows(k, d):
-        pltpu.make_async_copy(
-            gath.at[d, :, cols(k)],
-            rows_out.at[pl.ds(pl.multiple_of(d * rows, rows), rows), cols(k)],
-            rows_sem,
-        ).start()
 
     for k in range(gathers):
         span = cols(k)
@@ -164,28 +161,20 @@
         second = new_two / (1.0 - 0.95**10)
         held = mas_v[:, span]
         new_master = held - 0.05 * (first / (jnp.sqrt(second) + 1e-08) + 0.1 * held)
-        gath[dp, :, span] = new_master.astype(jnp.bfloat16)
+        rows_out[rows_of(dp), span] = new_master.astype(jnp.bfloat16)
         for q in others:
             direct(k, chip, q).start()
         relay(k, chip, core).start()
-        put_rows(k, dp)
-        one_v[:, span] = new_one
-        two_v[:, span] = new_two
-        mas_v[:, span] = new_master
-    outs = []
-    for i, (src, dst) in enumerate(((mas_v, mas_out), (one_v, one_out), (two_v, two_out))):
-        out = pltpu.make_async_copy(src, dst, out_sem.at[i])
-        out.start()
-        outs.append(out)
+        one_out[:, span] = new_one
+        two_out[:, span] = new_two
+        mas_out[:, span] = new_master
     for k in range(gathers):
         for q in others:
             direct(k, q, q).wait_recv()
             relay(k, q, core).start()
-            put_rows(k, 2 * q + core)
     for k in range(gathers):
         for q in [chip] + others:
             relay(k, q, other).wait_recv()
-            put_rows(k, 2 * q + other)
 
     for j in range(chunks):
         pair_copy(j).wait_send()
@@ -197,9 +186,15 @@
             direct(k, chip, q).wait_send()
             relay(k, q, core).wait_send()
         relay(k, chip, core).wait_send()
-    for out in outs:
-        out.wait()
-    pltpu.make_async_copy(rows_out, rows_out, rows_sem).wait()
+
+
+def write_out(*refs):
+    sems = refs[8]
+    copies = [pltpu.make_async_copy(refs[i], refs[4 + i], sems.at[i]) for i in range(4)]
+    for copy in copies:
+        copy.start()
+    for copy in copies:
+        copy.wait()
 
 
 def shards(n, depth, hidden, logit_grad, master, moment_one, moment_two):
@@ -211,14 +206,17 @@
     gathers = pieces(width, GATHER_CHUNKS)
     wc = width // chunks
     f32, bf16 = jnp.float32, jnp.bfloat16
-    state = jax.ShapeDtypeStruct((rows, width), f32)
+    state = ((rows, width), f32)
+    shapes = (((slab, width), bf16), state, state, state)
+    kept = slab * width * 2 + 3 * rows * width * 4
     dma = pltpu.SemaphoreType.DMA
     anywhere = pl.BlockSpec(memory_space=pl.ANY)
-    return pl.pallas_call(
+    in_vmem = pl.BlockSpec(memory_space=pltpu.VMEM)
+    held = pl.pallas_call(
         functools.partial(kernel, n, depth, chunks, gathers),
-        out_shape=(jax.ShapeDtypeStruct((slab, width), bf16), state, state, state),
+        out_shape=tuple(pltpu.VMEM(*shape) for shape in shapes),
         in_specs=[anywhere] * 5,
-        out_specs=(anywhere,) * 4,
+        out_specs=(in_vmem,) * 4,
         scratch_shapes=[
             pltpu.VMEM((tokens, slab), bf16),
             pltpu.VMEM((slab, tokens), bf16),
@@ -232,7 +230,6 @@
             pltpu.VMEM((chunks, chips, rows, wc), bf16),
             pltpu.VMEM((rows, width), f32),
             pltpu.VMEM((n * depth, 1, 128), f32),
-            pltpu.VMEM((n, rows, width), bf16),
             dma((chunks,)),
             dma,
             dma((3,)),
@@ -246,13 +243,19 @@
             dma((gathers, chips)),
             dma((gathers, chips)),
             dma((gathers, chips)),
-            dma,
-            dma((3,)),
         ],
         compiler_params=pltpu.CompilerParams(
-            collective_id=0, has_side_effects=True, vmem_limit_bytes=60 * 1024 * 1024
+            collective_id=0, has_side_effects=True, vmem_limit_bytes=VMEM_BYTES - kept - 96 * 1024
         ),
     )(hidden, logit_grad, master, moment_one, moment_two)
+    return pl.pallas_call(
+        write_out,
+        out_shape=tuple(pltpu.HBM(*shape) for shape in shapes),
+        in_specs=[anywhere] * 4,
+        out_specs=(anywhere,) * 4,
+        scratch_shapes=[dma((4,))],
+        compiler_params=pltpu.CompilerParams(vmem_limit_bytes=1024 * 1024),
+    )(*held)
 
 
 def solution(mesh):

time: 40 us -> 33.3 us (0.83); the launches traced: 39.2 us -> 33.1 us
  local copies, waits for them, and re-layouts: 7.31 us -> 0 us
  Pallas kernels: 31.3 us -> 32.5 us
    unnamed x4 -> x0, local copies, waits for them, and re-layouts: 7.31 us -> none
    pallas_call x0 -> x1, Pallas kernels: none -> 1.26 us  [shards(): pl.pallas_call(write_out, out_shape=tuple((pltpu.HBM(*shape) for shape in...]
where the time goes in v2:
time: 33.3 us; the launch traced here: 33.1 us
  Pallas kernels  32.5 us (98%)
  between operations  0.64 us (2%)
    pallas_call x1, Pallas kernels, shards(): pl.pallas_call(functools.partial(kernel, n, depth, chunks, gathers), out_...  31.2 us
    pallas_call x1, Pallas kernels, shards(): pl.pallas_call(write_out, out_shape=tuple((pltpu.HBM(*shape) for shape in...  1.26 us

profile of v2, /device:TPU:0, one launch (start us, length us, event | category | flops | bytes accessed | tf_op | source)
XLA Modules:
  0.0 33.1 jit_solution(9134755845285284766)
XLA Ops:
  0.6 31.2 %shard_map.84 = (bf16[256,2048]{1,0:T(8,128)(2,1)S(1)}, f32[32,2048]{1,0:T(8,128)S(1)}, f32[32,2048]{1,0:T(8,128)S(1)}, f32[32,2048]{1,0:T(8,128)S(1)}) custom-call(bf16[2048,2048]{1,0:T(8,128)(2,1)} %hid.1, bf16[2048,256]{1,0:T(8,128)(2,1)} %lgr.1, f32[32,2048]{1,0:T(8,128)} %mas.1, f32[32,2048]{1,0:T(8,128)} %one.1, f32[32,2048]{1,0:T(8,128)} %two.1), custom_call_target="tpu_custom_call" | custom-call | tf_op jit(solution)/shard_map/pallas_call | solution.py:215
  31.9 1.3 %shard_map.85 = (bf16[256,2048]{1,0:T(8,128)(2,1)}, f32[32,2048]{1,0:T(8,128)}, f32[32,2048]{1,0:T(8,128)}, f32[32,2048]{1,0:T(8,128)}) custom-call(bf16[256,2048]{1,0:T(8,128)(2,1)S(1)} %get-tuple-element.8.refs_0_, f32[32,2048]{1,0:T(8,128)S(1)} %get-tuple-element.9.refs_1_, f32[32,2048]{1,0:T(8,128)S(1)} %get-tuple-element.10.refs_2_, ...), custom_call_target="tpu_custom_call" | custom-call | tf_op jit(solution)/shard_map/pallas_call | solution.py:251
